TPU v7x, 32 devices: a whole 2x2x4 slice. The times are simulated.
32 devices in a mesh: grp: 2 (over x), az: 8 (over z, y), ax: 2 (over core).
Axes of the slice: x: 2, y: 2, z: 4, core: 2. Of those that a mesh axis runs over, the one named last changes fastest.
Arguments:
- cavity_block: float32 [8, 96, 32, 256], P(None, 'grp', 'az', 'ax'), may hold values from -95 to 95
- shell_block: float32 [8, 6, 32, 256], P(None, None, 'az', 'ax'), may hold values from -95 to 95
- column_matrix: float32 [2, 48, 48], P('grp'), may hold values from -2 to 6, as said below
- shell_matrix: float32 [6, 6], replicated, may hold values from -2 to 6, as said below
- shifted_diagonal: float32 [96, 32, 256], P('grp', 'az', 'ax'), may hold values from 1.6 to 3
- shell_diagonal: float32 [6, 32, 256], P(None, 'az', 'ax'), may hold values from 1.6 to 3
- wet_area: float32 [32, 256], P('az', 'ax'), may hold values from 0.3 to 1.5
Outputs:
- cavity_solution: float32 [8, 96, 32, 256], P(None, 'grp', 'az', 'ax')
- cavity_residual: float32 [8, 96, 32, 256], P(None, 'grp', 'az', 'ax')
- shell_solution: float32 [8, 6, 32, 256], P(None, None, 'az', 'ax')
- shell_residual: float32 [8, 6, 32, 256], P(None, None, 'az', 'ax')
Inputs may be any that keep to these rules, and one draw needn't show every extreme that they name: `column_matrix`: each symmetric and positive definite. `shell_matrix`: symmetric and positive definite.
All inputs are finite; a program needn't handle non-finite values.
Results may differ from a plain program's by a relative error of at most 0.0015.
Values sent between devices are 32-bit elements; how exact they have to be, the bound alone decides.
No kernel may reach another device: no remote copies, remote signals or barrier semaphores. Data moves between devices by JAX's collectives and lax.ppermute only.
A program may use at most 128 MiB of HBM per device.

v0:
```python
import jax
import jax.numpy as jnp
from jax import lax
from jax.sharding import PartitionSpec as P

ITERS = 3
exact_mode = lax.Precision.HIGHEST


def swapped(block, axis, apart):
    count = lax.axis_size(axis)
    route = []
    for low in range(count):
        high = low | 1 << apart
        if high != low and high < count:
            route += [(low, high), (high, low)]
    return lax.ppermute(block, axis, route)


def extended(array, sides, width, wrap):
    for axis, dim in sides:
        peers, length = (lax.axis_size(axis), array.shape[dim])
        up = [(i, (i + 1) % peers) for i in range(peers if wrap else peers - 1)]
        down = [(j, i) for i, j in up]
        last = lax.slice_in_dim(array, length - width, length, axis=dim)
        first = lax.slice_in_dim(array, 0, width, axis=dim)
        before = lax.ppermute(last, axis, up)
        after = lax.ppermute(first, axis, down)
        array = jnp.concatenate([before, array, after], axis=dim)
    return array


def solve_posdef(gram_matrix, targets):
    factor = jnp.linalg.cholesky(gram_matrix)
    middle = lax.linalg.triangular_solve(factor, targets, left_side=True, lower=True)
    return lax.linalg.triangular_solve(factor, middle, left_side=True, lower=True, transpose_a=True)


def products(first_set, second_set):
    return jnp.einsum("vrax,wrax->vw", first_set, second_set, precision=exact_mode)


def combine(vector_set, mixing):
    return jnp.einsum("vrax,vw->wrax", vector_set, mixing, precision=exact_mode)


def column_part(vector_set, matrix):
    flat_set = vector_set.reshape(vector_set.shape[0], vector_set.shape[1], -1)
    mixed_set = jnp.einsum("rs,vsc->vrc", matrix, flat_set, precision=exact_mode)
    return mixed_set.reshape(vector_set.shape)


def coupled(result, vector_set, wet_area, layout):
    half, interface_row, outer_flag = layout
    iface_own = lax.dynamic_slice_in_dim(vector_set, interface_row, 1, 1)
    wall_own = vector_set[:, half - 1 : half]
    sent = jnp.concatenate([iface_own, wall_own], axis=1)
    received = swapped(sent, "grp", 0)
    result_row = lax.dynamic_slice_in_dim(result, interface_row, 1, 1)
    result = lax.dynamic_update_slice_in_dim(
        result, result_row - received[:, 0:1], interface_row, 1
    )
    wall = outer_flag * wall_own + (1.0 - outer_flag) * received[:, 1:2]
    shell_top = vector_set[:, half : half + 1]
    result = result.at[:, half - 1 : half].add(-outer_flag * wet_area * shell_top)
    result = result.at[:, half : half + 1].add(-wet_area * wall)
    return result


def apply_shallow(vector_set, matrix, diagonal_set, wet_area, layout):
    beside_all = extended(vector_set, (("az", 2),), 1, True)
    along = extended(vector_set, (("ax", 3),), 1, False)
    neighbours = beside_all[:, :, 2:] + beside_all[:, :, :-2] + along[..., 2:] + along[..., :-2]
    result = column_part(vector_set, matrix) + (4.0 + diagonal_set) * vector_set - neighbours
    return coupled(result, vector_set, wet_area, layout)


def per_device(
    cavity_block,
    shell_block,
    column_matrix,
    shell_matrix,
    shifted_diagonal,
    shell_diagonal,
    wet_area,
):
    group_index = lax.axis_index("grp")
    outer_flag = (group_index == 1).astype(jnp.float32)
    shell_share = 1.0 - outer_flag
    half = column_matrix.shape[1]
    shell_rows = shell_matrix.shape[0]
    interface_row = jnp.where(group_index == 1, 0, half - 1).astype(jnp.int32)
    layout = (half, interface_row, outer_flag)
    upper = jnp.concatenate([column_matrix[0], jnp.zeros((half, shell_rows), jnp.float32)], axis=1)
    lower = jnp.concatenate([jnp.zeros((shell_rows, half), jnp.float32), shell_matrix], axis=1)
    matrix = jnp.concatenate([upper, lower], axis=0)
    right_side = jnp.concatenate([cavity_block, shell_block], axis=1)
    diagonal_own = jnp.concatenate([shifted_diagonal, shell_diagonal], axis=0)

    def moments_local(first_set, second_set):
        cavity_part = products(first_set[:, :half], second_set[:, :half])
        return cavity_part + shell_share * products(first_set[:, half:], second_set[:, half:])

    residual = right_side
    direction = right_side
    solution = jnp.zeros_like(right_side)
    start_core = residual
    norms_now = lax.psum(moments_local(start_core, start_core), ("grp", "az", "ax"))
    for sweep in range(ITERS):
        image_set = apply_shallow(direction, matrix, diagonal_own, wet_area, layout)
        direction_core = direction
        residual_core = residual
        curvature, crossing, squares = lax.psum(
            (
                moments_local(direction_core, image_set),
                moments_local(image_set, residual_core),
                moments_local(image_set, image_set),
            ),
            ("grp", "az", "ax"),
        )
        step_mix = solve_posdef(curvature, norms_now)
        norms_next = norms_now - jnp.dot(step_mix.T, crossing, precision=exact_mode)
        norms_next = norms_next - jnp.dot(crossing.T, step_mix, precision=exact_mode)
        norms_next = norms_next + jnp.dot(
            jnp.dot(step_mix.T, squares, precision=exact_mode), step_mix, precision=exact_mode
        )
        solution = solution + combine(direction_core, step_mix)
        residual = residual - combine(image_set, step_mix)
        if sweep + 1 < ITERS:
            turn_mix = solve_posdef(norms_now, norms_next)
            direction = residual + combine(direction, turn_mix)
            norms_now = norms_next
    return (solution[:, :half], residual[:, :half], solution[:, half:], residual[:, half:])


def solution(mesh):
    return jax.shard_map(
        per_device,
        mesh=mesh,
        in_specs=(
            P(None, "grp", "az", "ax"),
            P(None, None, "az", "ax"),
            P("grp", None, None),
            P(),
            P("grp", "az", "ax"),
            P(None, "az", "ax"),
            P("az", "ax"),
        ),
        out_specs=(
            P(None, "grp", "az", "ax"),
            P(None, "grp", "az", "ax"),
            P(None, None, "az", "ax"),
            P(None, None, "az", "ax"),
        ),
        check_vma=False,
    )
```

profile of v0, /device:TPU:0, one launch (start us, length us, event | category | flops | bytes accessed | tf_op | source)
XLA Modules:
  0.0 250.7 jit_solution(17498085943303923312)
XLA Ops:
  0.6 2.5 fusion.124
  5.1 2.4 collective-permute-start.3
  10.0 2.3 collective-permute-start.1
  12.3 3.0 %collective-permute-start = (f32[8,54,1,128]{3,0,1,2:T(8,128)}, f32[8,54,1,128]{3,0,1,2:T(8,128)}, u32[]{:S(2)}, u32[]{:S(2)}) collective-permute-start(f32[8,54,1,128]{3,0,1,2:T(8,128)} %get-tuple-element.110), channel_id=1, source_target_pairs={{2,0},{4,2},{6,4},{8,6},{10,8},{12,10},{14,12},{0,14},{3,1},{5,3},... | collective-permute-start | bytes 663560 | tf_op jit(solution)/shard_map/ppermute | solution.py:28
  18.4 1.9 convolution_bitcast_fusion.3
  21.4 2.4 convolution_bitcast_fusion.2
  26.3 2.5 fusion.26
  35.7 38.6 %all-reduce.3 = (f32[8,8]{0,1:T(8,128)S(1)}, f32[8,8]{1,0:T(8,128)S(1)}, f32[8,8]{0,1:T(8,128)S(1)}, f32[8,8]{0,1:T(8,128)S(1)}) all-reduce(f32[8,8]{0,1:T(8,128)S(1)} %copy-done.18, f32[8,8]{1,0:T(8,128)S(1)} %bitcast.241, f32[8,8]{0,1:T(8,128)S(1)} %fusion.11, ...), channel_id=1, replica_groups=mesh['grp'=2,'az'=8,'ax'=2] {'grp','az','ax'}, use_global_device_ids=true, to_apply=%region_3.0 | all-reduce | flops 256 | bytes 2048 | tf_op jit(solution)/shard_map/psum | solution.py:108
  77.5 1.9 fusion.31
  88.4 2.1 copy.206
  94.7 2.4 collective-permute-start.6
  97.1 2.4 collective-permute-start.5
  99.5 3.1 %convolution_bitcast_fusion.1 = f32[8,54,512]{2,1,0:T(8,128)} fusion(f32[8,54,512]{2,0,1:T(8,128)S(1)} %bitcast.235, f32[6,6]{1,0:T(8,128)S(1)} %copy-done.14, f32[48,48]{1,0:T(8,128)} %bitcast.238), kind=kOutput, calls=%fused_computation.1 | convolution fusion | flops 143341808 | bytes 1778832 | tf_op jit(solution)/shard_map/rs,vsc->vrc/dot_general | solution.py:49
  103.3 2.3 collective-permute-start.9
  112.0 2.5 fusion.22
  122.3 37.7 %all-reduce.2 = (f32[8,8]{0,1:T(8,128)S(1)}, f32[8,8]{0,1:T(8,128)}, f32[8,8]{0,1:T(8,128)}) all-reduce(f32[8,8]{0,1:T(8,128)S(1)} %fusion.7, f32[8,8]{0,1:T(8,128)S(1)} %fusion.5, f32[8,8]{0,1:T(8,128)S(1)} %fusion.3), channel_id=1, replica_groups=mesh['grp'=2,'az'=8,'ax'=2] {'grp','az','ax'}, use_global_device_ids=true, to_apply=%region_6.10 | all-reduce | flops 192 | bytes 1536 | tf_op jit(solution)/shard_map/psum | solution.py:113
  172.1 2.2 copy.237
  174.4 2.0 collective-permute-start.13
  178.6 2.7 %collective-permute-start.11 = (f32[8,54,1,128]{3,0,1,2:T(8,128)}, f32[8,54,1,128]{3,0,1,2:T(8,128)S(1)}, u32[]{:S(2)}, u32[]{:S(2)}) collective-permute-start(f32[8,54,1,128]{3,0,1,2:T(8,128)} %get-tuple-element.101), channel_id=1, source_target_pairs={{0,2},{2,4},{4,6},{6,8},{8,10},{10,12},{12,14},{14,0},{1,3},{3,5},... | collective-permute-start | bytes 663560 | tf_op jit(solution)/shard_map/ppermute | solution.py:27
  181.3 2.1 collective-permute-start.10
  183.4 3.1 %convolution_bitcast_fusion = f32[8,54,512]{2,1,0:T(8,128)} fusion(f32[8,54,512]{2,0,1:T(8,128)S(1)} %bitcast.236, f32[6,6]{1,0:T(8,128)S(1)} %copy-done.14, f32[48,48]{1,0:T(8,128)} %bitcast.239), kind=kOutput, calls=%fused_computation | convolution fusion | flops 143341808 | bytes 1778832 | tf_op jit(solution)/shard_map/rs,vsc->vrc/dot_general | solution.py:49
  187.1 2.2 collective-permute-start.14
  194.5 2.4 fusion.18
  200.5 38.7 %psum.63 = f32[8,8]{0,1:T(8,128)S(1)} all-reduce(f32[8,8]{0,1:T(8,128)S(1)} %fusion.1), channel_id=1, replica_groups=mesh['grp'=2,'az'=8,'ax'=2] {'grp','az','ax'}, use_global_device_ids=true, to_apply=%region_9.13 | all-reduce | flops 64 | bytes 512 | tf_op jit(solution)/shard_map/psum | solution.py:113
  (189 shorter events, 84.2 us)
Async XLA Ops:
  0.6 2.5 %copy-start.6 = (f32[8,6,4,128]{3,2,1,0:T(4,128)S(1)}, f32[8,6,4,128]{3,2,1,0:T(4,128)}, u32[]{:S(2)}) copy-start(f32[8,6,4,128]{3,2,1,0:T(4,128)} %param.25) | copy-start | bytes 294916
  5.1 19.4 %collective-permute-start.3 = (f32[8,54,4,1]{1,0,3,2:T(8,128)}, f32[8,54,4,1]{1,0,3,2:T(8,128)S(1)}, u32[]{:S(2)}, u32[]{:S(2)}) collective-permute-start(f32[8,54,4,1]{1,0,3,2:T(8,128)} %copy.166), channel_id=1, source_target_pairs={{0,1},{2,3},{4,5},{6,7},{8,9},{10,11},{12,13},{14,15},{16,17},{18,... | collective-permute-start | bytes 20744 | tf_op jit(solution)/shard_map/ppermute | solution.py:27
  7.5 10.9 %copy-start = (f32[8,48,4,128]{3,2,1,0:T(4,128)S(1)}, f32[8,48,4,128]{3,2,1,0:T(4,128)}, u32[]{:S(2)}) copy-start(f32[8,48,4,128]{3,2,1,0:T(4,128)} %param.24) | copy-start | bytes 2359300
  7.9 17.0 %collective-permute-start.2 = (f32[8,54,4,1]{1,0,3,2:T(8,128)S(1)}, f32[8,54,4,1]{1,0,3,2:T(8,128)S(1)}, u32[]{:S(2)}, u32[]{:S(2)}) collective-permute-start(f32[8,54,4,1]{1,0,3,2:T(8,128)S(1)} %copy.164), channel_id=1, source_target_pairs={{1,0},{3,2},{5,4},{7,6},{9,8},{11,10},{13,12},{15,14},{17,16},{19,... | collective-permute-start | bytes 20744 | tf_op jit(solution)/shard_map/ppermute | solution.py:28
  10.0 16.3 %collective-permute-start.1 = (f32[8,54,1,128]{3,0,1,2:T(8,128)}, f32[8,54,1,128]{3,0,1,2:T(8,128)}, u32[]{:S(2)}, u32[]{:S(2)}) collective-permute-start(f32[8,54,1,128]{3,0,1,2:T(8,128)} %get-tuple-element.111), channel_id=1, source_target_pairs={{0,2},{2,4},{4,6},{6,8},{8,10},{10,12},{12,14},{14,0},{1,3},{3,5},... | collective-permute-start | bytes 663560 | tf_op jit(solution)/shard_map/ppermute | solution.py:27
  12.3 14.0 %collective-permute-start = (f32[8,54,1,128]{3,0,1,2:T(8,128)}, f32[8,54,1,128]{3,0,1,2:T(8,128)}, u32[]{:S(2)}, u32[]{:S(2)}) collective-permute-start(f32[8,54,1,128]{3,0,1,2:T(8,128)} %get-tuple-element.110), channel_id=1, source_target_pairs={{2,0},{4,2},{6,4},{8,6},{10,8},{12,10},{14,12},{0,14},{3,1},{5,3},... | collective-permute-start | bytes 663560 | tf_op jit(solution)/shard_map/ppermute | solution.py:28
  16.7 12.1 %collective-permute-start.4 = (f32[8,2,4,128]{3,0,1,2:T(8,128)}, f32[8,2,4,128]{3,0,1,2:T(8,128)}, u32[]{:S(2)}, u32[]{:S(2)}) collective-permute-start(f32[8,2,4,128]{3,0,1,2:T(8,128)} %pad_maximum_fusion.12), channel_id=1, source_target_pairs={{0,16},{16,0},{1,17},{17,1},{2,18},{18,2},{3,19},{19,3},{4,20},{20... | collective-permute-start | bytes 98312 | tf_op jit(solution)/shard_map/ppermute | solution.py:17
  21.3 2.4 copy-start.21
  21.3 2.4 copy-start.11
  21.4 2.4 copy-start.19
  90.6 18.3 %collective-permute-start.8 = (f32[8,54,4,1]{1,0,3,2:T(8,128)}, f32[8,54,4,1]{1,0,3,2:T(8,128)}, u32[]{:S(2)}, u32[]{:S(2)}) collective-permute-start(f32[8,54,4,1]{1,0,3,2:T(8,128)} %copy.206), channel_id=1, source_target_pairs={{0,1},{2,3},{4,5},{6,7},{8,9},{10,11},{12,13},{14,15},{16,17},{18,... | collective-permute-start | bytes 20744 | tf_op jit(solution)/shard_map/ppermute | solution.py:27
  93.4 16.6 %collective-permute-start.7 = (f32[8,54,4,1]{1,0,3,2:T(8,128)}, f32[8,54,4,1]{1,0,3,2:T(8,128)S(1)}, u32[]{:S(2)}, u32[]{:S(2)}) collective-permute-start(f32[8,54,4,1]{1,0,3,2:T(8,128)} %copy.204), channel_id=1, source_target_pairs={{1,0},{3,2},{5,4},{7,6},{9,8},{11,10},{13,12},{15,14},{17,16},{19,... | collective-permute-start | bytes 20744 | tf_op jit(solution)/shard_map/ppermute | solution.py:28
  94.7 16.6 %collective-permute-start.6 = (f32[8,54,1,128]{3,0,1,2:T(8,128)}, f32[8,54,1,128]{3,0,1,2:T(8,128)S(1)}, u32[]{:S(2)}, u32[]{:S(2)}) collective-permute-start(f32[8,54,1,128]{3,0,1,2:T(8,128)} %get-tuple-element.107), channel_id=1, source_target_pairs={{0,2},{2,4},{4,6},{6,8},{8,10},{10,12},{12,14},{14,0},{1,3},{3,5},... | collective-permute-start | bytes 663560 | tf_op jit(solution)/shard_map/ppermute | solution.py:27
  97.1 14.9 %collective-permute-start.5 = (f32[8,54,1,128]{3,0,1,2:T(8,128)}, f32[8,54,1,128]{3,0,1,2:T(8,128)}, u32[]{:S(2)}, u32[]{:S(2)}) collective-permute-start(f32[8,54,1,128]{3,0,1,2:T(8,128)} %get-tuple-element.106), channel_id=1, source_target_pairs={{2,0},{4,2},{6,4},{8,6},{10,8},{12,10},{14,12},{0,14},{3,1},{5,3},... | collective-permute-start | bytes 663560 | tf_op jit(solution)/shard_map/ppermute | solution.py:28
  99.5 3.2 %copy-start.12 = (f32[8,1,4,128]{3,0,1,2:T(8,128)S(1)}, f32[8,1,4,128]{3,0,1,2:T(8,128)}, u32[]{:S(2)}) copy-start(f32[8,1,4,128]{3,0,1,2:T(8,128)} %get-tuple-element.104) | copy-start | bytes 49156
  99.5 3.2 %copy-start.13 = (f32[8,1,4,128]{3,0,1,2:T(8,128)S(1)}, f32[8,1,4,128]{3,0,1,2:T(8,128)}, u32[]{:S(2)}) copy-start(f32[8,1,4,128]{3,0,1,2:T(8,128)} %get-tuple-element.105) | copy-start | bytes 49156
  102.7 2.9 %copy-start.16 = (f32[8,8]{1,0:T(8,128)S(1)}, f32[8,8]{1,0:T(8,128)}, u32[]{:S(2)}) copy-start(f32[8,8]{1,0:T(8,128)} %copy.218) | copy-start | bytes 772
  103.3 11.2 %collective-permute-start.9 = (f32[8,2,4,128]{3,0,1,2:T(8,128)}, f32[8,2,4,128]{3,0,1,2:T(8,128)}, u32[]{:S(2)}, u32[]{:S(2)}) collective-permute-start(f32[8,2,4,128]{3,0,1,2:T(8,128)} %pad_maximum_fusion.13), channel_id=1, source_target_pairs={{0,16},{16,0},{1,17},{17,1},{2,18},{18,2},{3,19},{19,3},{4,20},{20... | collective-permute-start | bytes 98312 | tf_op jit(solution)/shard_map/ppermute | solution.py:17
  172.1 4.2 %copy-start.1 = (f32[8,54,4,1]{3,0,1,2:T(8,128)S(1)}, f32[8,54,4,1]{3,0,1,2:T(8,128)}, u32[]{:S(2)}) copy-start(f32[8,54,4,1]{3,0,1,2:T(8,128)} %get-tuple-element.102) | copy-start | bytes 20740
  174.4 15.0 %collective-permute-start.13 = (f32[8,54,4,1]{1,0,3,2:T(8,128)}, f32[8,54,4,1]{1,0,3,2:T(8,128)}, u32[]{:S(2)}, u32[]{:S(2)}) collective-permute-start(f32[8,54,4,1]{1,0,3,2:T(8,128)} %copy.237), channel_id=1, source_target_pairs={{0,1},{2,3},{4,5},{6,7},{8,9},{10,11},{12,13},{14,15},{16,17},{18,... | collective-permute-start | bytes 20744 | tf_op jit(solution)/shard_map/ppermute | solution.py:27
  177.3 13.2 %collective-permute-start.12 = (f32[8,54,4,1]{1,0,3,2:T(8,128)}, f32[8,54,4,1]{1,0,3,2:T(8,128)S(1)}, u32[]{:S(2)}, u32[]{:S(2)}) collective-permute-start(f32[8,54,4,1]{1,0,3,2:T(8,128)} %copy.235), channel_id=1, source_target_pairs={{1,0},{3,2},{5,4},{7,6},{9,8},{11,10},{13,12},{15,14},{17,16},{19,... | collective-permute-start | bytes 20744 | tf_op jit(solution)/shard_map/ppermute | solution.py:28
  178.6 13.4 %collective-permute-start.11 = (f32[8,54,1,128]{3,0,1,2:T(8,128)}, f32[8,54,1,128]{3,0,1,2:T(8,128)S(1)}, u32[]{:S(2)}, u32[]{:S(2)}) collective-permute-start(f32[8,54,1,128]{3,0,1,2:T(8,128)} %get-tuple-element.101), channel_id=1, source_target_pairs={{0,2},{2,4},{4,6},{6,8},{8,10},{10,12},{12,14},{14,0},{1,3},{3,5},... | collective-permute-start | bytes 663560 | tf_op jit(solution)/shard_map/ppermute | solution.py:27
  181.3 13.2 %collective-permute-start.10 = (f32[8,54,1,128]{3,0,1,2:T(8,128)}, f32[8,54,1,128]{3,0,1,2:T(8,128)}, u32[]{:S(2)}, u32[]{:S(2)}) collective-permute-start(f32[8,54,1,128]{3,0,1,2:T(8,128)} %get-tuple-element.100), channel_id=1, source_target_pairs={{2,0},{4,2},{6,4},{8,6},{10,8},{12,10},{14,12},{0,14},{3,1},{5,3},... | collective-permute-start | bytes 663560 | tf_op jit(solution)/shard_map/ppermute | solution.py:28
  187.1 9.8 %collective-permute-start.14 = (f32[8,2,4,128]{3,0,1,2:T(8,128)}, f32[8,2,4,128]{3,0,1,2:T(8,128)}, u32[]{:S(2)}, u32[]{:S(2)}) collective-permute-start(f32[8,2,4,128]{3,0,1,2:T(8,128)} %pad_maximum_fusion.14), channel_id=1, source_target_pairs={{0,16},{16,0},{1,17},{17,1},{2,18},{18,2},{3,19},{19,3},{4,20},{20... | collective-permute-start | bytes 98312 | tf_op jit(solution)/shard_map/ppermute | solution.py:17
  (17 other events, 17.9 us)
where the time goes:
time: 252 us; the launch traced here: 251 us
  blocking collectives  115 us (46%)
  local copies, waits for them, and re-layouts  36.6 us (15%)
  matrix products  36.5 us (14%)
  starting transfers between devices  31.1 us (12%)
  other arithmetic  28.4 us (11%)
    psum x2, blocking collectives, per_device(): lax.psum((moments_local(direction_core, image_set), moments_local(image_s...  76.4 us
    psum x1, blocking collectives, per_device(): lax.psum(moments_local(start_core, start_core), ('grp', 'az', 'ax'))  38.6 us
    dot_general x14, matrix products, products(): jnp.einsum('vrax,wrax->vw', first_set, second_set, precision=exact_mode)  15.5 us
    ppermute x6, starting transfers between devices, extended(): before = lax.ppermute(last, axis, up)  13.6 us
    unnamed x50, local copies, waits for them, and re-layouts  12 us
    ppermute x6, starting transfers between devices, extended(): after = lax.ppermute(first, axis, down)  11.4 us
    dot_general x8, matrix products, combine(): return jnp.einsum('vrax,vw->wrax', vector_set, mixing, precision=exact_mode)  9.04 us
    dot_general x3, matrix products, column_part(): jnp.einsum('rs,vsc->vrc', matrix, flat_set, precision=exact_mode)  8.66 us
  transfers between devices with their start and end apart: 15, of which 2 were waited for; matrix products, arithmetic and copies ran while one was open for 14% of the time, Pallas kernels for 0%

commit v1 on v0

--- a/solution.py
+++ b/solution.py
@@ -105,7 +105,9 @@
     direction = right_side
     solution = jnp.zeros_like(right_side)
     start_core = residual
-    norms_now = lax.psum(moments_local(start_core, start_core), ("grp", "az", "ax"))
+    part = moments_local(start_core, start_core)
+    terms = lax.all_gather(part, ("grp", "az", "ax"))
+    norms_now = jnp.sum(terms, axis=0)
     for sweep in range(ITERS):
         image_set = apply_shallow(direction, matrix, diagonal_own, wet_area, layout)
         direction_core = direction

time: 252 us -> 291 us (1.15)
  blocking collectives: 115 us -> 153 us
    psum x1 -> x0, blocking collectives: 38.6 us -> none  [per_device(): lax.psum(moments_local(start_core, start_core), ('grp', 'az', 'ax'))]
    all_gather x0 -> x1, blocking collectives: none -> 38.5 us  [per_device(): terms = lax.all_gather(part, ('grp', 'az', 'ax'))]
    psum x2 -> x3, blocking collectives: 76.4 us -> 114 us  [per_device(): lax.psum((moments_local(direction_core, image_set), moments_local(image_s...]
    unnamed x50 -> x57, local copies, waits for them, and re-layouts: 12 us -> 12.9 us
  transfers between devices with their start and end apart: 15 -> 15, of which waited for: 2 -> 2; matrix products, arithmetic and copies ran while one was open for 14% -> 13% of each run, Pallas kernels for 0% -> 0%
where the time goes in v1:
time: 291 us; the launch traced here: 289 us
  blocking collectives  153 us (53%)
  local copies, waits for them, and re-layouts  37 us (13%)
  matrix products  35.8 us (12%)
  starting transfers between devices  31.2 us (11%)
  other arithmetic  29 us (10%)
    psum x3, blocking collectives, per_device(): lax.psum((moments_local(direction_core, image_set), moments_local(image_s...  114 us
    all_gather x1, blocking collectives, per_device(): terms = lax.all_gather(part, ('grp', 'az', 'ax'))  38.5 us
    dot_general x14, matrix products, products(): jnp.einsum('vrax,wrax->vw', first_set, second_set, precision=exact_mode)  14.9 us
    ppermute x6, starting transfers between devices, extended(): before = lax.ppermute(last, axis, up)  13.6 us
    unnamed x57, local copies, waits for them, and re-layouts  12.9 us
    ppermute x6, starting transfers between devices, extended(): after = lax.ppermute(first, axis, down)  11.5 us
    dot_general x8, matrix products, combine(): return jnp.einsum('vrax,vw->wrax', vector_set, mixing, precision=exact_mode)  9.04 us
    dot_general x3, matrix products, column_part(): jnp.einsum('rs,vsc->vrc', matrix, flat_set, precision=exact_mode)  8.67 us
  transfers between devices with their start and end apart: 15, of which 2 were waited for; matrix products, arithmetic and copies ran while one was open for 13% of the time, Pallas kernels for 0%

profile of v1, /device:TPU:0, one launch (start us, length us, event | category | flops | bytes accessed | tf_op | source)
XLA Modules:
  0.0 288.9 jit_solution(13106895905586489445)
XLA Ops:
  0.6 2.5 fusion.124
  5.1 2.4 collective-permute-start.3
  9.2 2.4 collective-permute-start.1
  11.6 3.1 %collective-permute-start = (f32[8,54,1,128]{3,0,1,2:T(8,128)S(1)}, f32[8,54,1,128]{3,0,1,2:T(8,128)}, u32[]{:S(2)}, u32[]{:S(2)}) collective-permute-start(f32[8,54,1,128]{3,0,1,2:T(8,128)S(1)} %get-tuple-element.109), channel_id=1, source_target_pairs={{2,0},{4,2},{6,4},{8,6},{10,8},{12,10},{14,12},{0,14},{3,1},{5,3},... | collective-permute-start | bytes 663560 | tf_op jit(solution)/shard_map/ppermute | solution.py:28
  17.7 1.9 convolution_bitcast_fusion.3
  20.0 38.5 %all-gather = f32[256,8]{1,0:T(8,128)S(1)} all-gather(f32[8,8]{1,0:T(8,128)S(1)} %copy.184), channel_id=2, replica_groups=mesh['grp'=2,'az'=8,'ax'=2] {'grp','az','ax'}, dimensions={0}, use_global_device_ids=true | all-gather | bytes 8448 | tf_op jit(solution)/shard_map/all_gather | solution.py:109
  60.9 2.4 convolution_bitcast_fusion.2
  68.6 2.3 fusion.26
  77.5 37.2 %all-reduce.3 = (f32[8,8]{1,0:T(8,128)S(1)}, f32[8,8]{0,1:T(8,128)S(1)}, f32[8,8]{0,1:T(8,128)S(1)}) all-reduce(f32[8,8]{1,0:T(8,128)S(1)} %bitcast.243, f32[8,8]{0,1:T(8,128)S(1)} %fusion.11, f32[8,8]{0,1:T(8,128)S(1)} %fusion.9), channel_id=1, replica_groups=mesh['grp'=2,'az'=8,'ax'=2] {'grp','az','ax'}, use_global_device_ids=true, to_apply=%region_0.1 | all-reduce | flops 192 | bytes 1536 | tf_op jit(solution)/shard_map/psum | solution.py:115
  125.9 2.1 copy.208
  132.2 2.3 collective-permute-start.6
  134.6 2.4 collective-permute-start.5
  137.0 3.1 %convolution_bitcast_fusion.1 = f32[8,54,512]{2,1,0:T(8,128)} fusion(f32[8,54,512]{2,0,1:T(8,128)S(1)} %bitcast.237, f32[6,6]{1,0:T(8,128)S(1)} %copy-done.16, f32[48,48]{1,0:T(8,128)} %bitcast.240), kind=kOutput, calls=%fused_computation.1 | convolution fusion | flops 143341808 | bytes 1778832 | tf_op jit(solution)/shard_map/rs,vsc->vrc/dot_general | solution.py:49
  140.8 2.3 collective-permute-start.9
  149.5 2.5 fusion.22
  159.8 39.2 %all-reduce.2 = (f32[8,8]{0,1:T(8,128)S(1)}, f32[8,8]{0,1:T(8,128)}, f32[8,8]{0,1:T(8,128)}) all-reduce(f32[8,8]{0,1:T(8,128)S(1)} %fusion.7, f32[8,8]{0,1:T(8,128)S(1)} %fusion.5, f32[8,8]{0,1:T(8,128)S(1)} %fusion.3), channel_id=1, replica_groups=mesh['grp'=2,'az'=8,'ax'=2] {'grp','az','ax'}, use_global_device_ids=true, to_apply=%region_6.10 | all-reduce | flops 192 | bytes 1536 | tf_op jit(solution)/shard_map/psum | solution.py:115
  211.2 2.2 copy.239
  213.4 2.0 collective-permute-start.13
  217.6 2.7 collective-permute-start.11
  220.3 2.1 collective-permute-start.10
  222.4 3.1 %convolution_bitcast_fusion = f32[8,54,512]{2,1,0:T(8,128)} fusion(f32[8,54,512]{2,0,1:T(8,128)S(1)} %bitcast.238, f32[6,6]{1,0:T(8,128)S(1)} %copy-done.16, f32[48,48]{1,0:T(8,128)} %bitcast.241), kind=kOutput, calls=%fused_computation | convolution fusion | flops 143341808 | bytes 1778832 | tf_op jit(solution)/shard_map/rs,vsc->vrc/dot_general | solution.py:49
  226.2 2.2 collective-permute-start.14
  233.6 2.4 fusion.18
  239.6 37.9 %psum.55 = f32[8,8]{0,1:T(8,128)S(1)} all-reduce(f32[8,8]{0,1:T(8,128)S(1)} %fusion.1), channel_id=1, replica_groups=mesh['grp'=2,'az'=8,'ax'=2] {'grp','az','ax'}, use_global_device_ids=true, to_apply=%region_9.13 | all-reduce | flops 64 | bytes 512 | tf_op jit(solution)/shard_map/psum | solution.py:115
  (198 shorter events, 86.5 us)
Async XLA Ops:
  0.6 2.5 copy-start.7
  5.1 60.1 %collective-permute-start.3 = (f32[8,54,4,1]{1,0,3,2:T(8,128)}, f32[8,54,4,1]{1,0,3,2:T(8,128)S(1)}, u32[]{:S(2)}, u32[]{:S(2)}) collective-permute-start(f32[8,54,4,1]{1,0,3,2:T(8,128)} %copy.166), channel_id=1, source_target_pairs={{0,1},{2,3},{4,5},{6,7},{8,9},{10,11},{12,13},{14,15},{16,17},{18,... | collective-permute-start | bytes 20744 | tf_op jit(solution)/shard_map/ppermute | solution.py:27
  7.5 10.2 %copy-start = (f32[8,48,4,128]{3,2,1,0:T(4,128)S(1)}, f32[8,48,4,128]{3,2,1,0:T(4,128)}, u32[]{:S(2)}) copy-start(f32[8,48,4,128]{3,2,1,0:T(4,128)} %param.24) | copy-start | bytes 2359300
  7.9 58.7 %collective-permute-start.2 = (f32[8,54,4,1]{1,0,3,2:T(8,128)S(1)}, f32[8,54,4,1]{1,0,3,2:T(8,128)S(1)}, u32[]{:S(2)}, u32[]{:S(2)}) collective-permute-start(f32[8,54,4,1]{1,0,3,2:T(8,128)S(1)} %copy.164), channel_id=1, source_target_pairs={{1,0},{3,2},{5,4},{7,6},{9,8},{11,10},{13,12},{15,14},{17,16},{19,... | collective-permute-start | bytes 20744 | tf_op jit(solution)/shard_map/ppermute | solution.py:28
  9.2 58.7 %collective-permute-start.1 = (f32[8,54,1,128]{3,0,1,2:T(8,128)S(1)}, f32[8,54,1,128]{3,0,1,2:T(8,128)S(1)}, u32[]{:S(2)}, u32[]{:S(2)}) collective-permute-start(f32[8,54,1,128]{3,0,1,2:T(8,128)S(1)} %get-tuple-element.110), channel_id=1, source_target_pairs={{0,2},{2,4},{4,6},{6,8},{8,10},{10,12},{12,14},{14,0},{1,3},{3,5},... | collective-permute-start | bytes 663560 | tf_op jit(solution)/shard_map/ppermute | solution.py:27
  11.6 57.0 %collective-permute-start = (f32[8,54,1,128]{3,0,1,2:T(8,128)S(1)}, f32[8,54,1,128]{3,0,1,2:T(8,128)}, u32[]{:S(2)}, u32[]{:S(2)}) collective-permute-start(f32[8,54,1,128]{3,0,1,2:T(8,128)S(1)} %get-tuple-element.109), channel_id=1, source_target_pairs={{2,0},{4,2},{6,4},{8,6},{10,8},{12,10},{14,12},{0,14},{3,1},{5,3},... | collective-permute-start | bytes 663560 | tf_op jit(solution)/shard_map/ppermute | solution.py:28
  16.1 54.9 %collective-permute-start.4 = (f32[8,2,4,128]{3,0,1,2:T(8,128)}, f32[8,2,4,128]{3,0,1,2:T(8,128)}, u32[]{:S(2)}, u32[]{:S(2)}) collective-permute-start(f32[8,2,4,128]{3,0,1,2:T(8,128)} %pad_maximum_fusion.12), channel_id=1, source_target_pairs={{0,16},{16,0},{1,17},{17,1},{2,18},{18,2},{3,19},{19,3},{4,20},{20... | collective-permute-start | bytes 98312 | tf_op jit(solution)/shard_map/ppermute | solution.py:17
  60.9 2.4 copy-start.24
  60.9 2.4 copy-start.13
  63.3 8.4 %copy-start.17 = (f32[4,128]{1,0:T(4,128)}, f32[4,128]{1,0:T(4,128)S(1)}, u32[]{:S(2)}) copy-start(f32[4,128]{1,0:T(4,128)S(1)} %get-tuple-element.118) | copy-start | bytes 6148
  64.0 4.6 %copy-start.1 = (f32[8,54,512]{2,1,0:T(8,128)S(1)}, f32[8,54,512]{2,1,0:T(8,128)}, u32[]{:S(2)}) copy-start(f32[8,54,512]{2,1,0:T(8,128)} %convolution_bitcast_fusion.2) | copy-start | bytes 2654212
  128.1 18.3 %collective-permute-start.8 = (f32[8,54,4,1]{1,0,3,2:T(8,128)}, f32[8,54,4,1]{1,0,3,2:T(8,128)}, u32[]{:S(2)}, u32[]{:S(2)}) collective-permute-start(f32[8,54,4,1]{1,0,3,2:T(8,128)} %copy.208), channel_id=1, source_target_pairs={{0,1},{2,3},{4,5},{6,7},{8,9},{10,11},{12,13},{14,15},{16,17},{18,... | collective-permute-start | bytes 20744 | tf_op jit(solution)/shard_map/ppermute | solution.py:27
  130.9 16.6 %collective-permute-start.7 = (f32[8,54,4,1]{1,0,3,2:T(8,128)}, f32[8,54,4,1]{1,0,3,2:T(8,128)S(1)}, u32[]{:S(2)}, u32[]{:S(2)}) collective-permute-start(f32[8,54,4,1]{1,0,3,2:T(8,128)} %copy.206), channel_id=1, source_target_pairs={{1,0},{3,2},{5,4},{7,6},{9,8},{11,10},{13,12},{15,14},{17,16},{19,... | collective-permute-start | bytes 20744 | tf_op jit(solution)/shard_map/ppermute | solution.py:28
  132.2 16.6 %collective-permute-start.6 = (f32[8,54,1,128]{3,0,1,2:T(8,128)}, f32[8,54,1,128]{3,0,1,2:T(8,128)S(1)}, u32[]{:S(2)}, u32[]{:S(2)}) collective-permute-start(f32[8,54,1,128]{3,0,1,2:T(8,128)} %get-tuple-element.106), channel_id=1, source_target_pairs={{0,2},{2,4},{4,6},{6,8},{8,10},{10,12},{12,14},{14,0},{1,3},{3,5},... | collective-permute-start | bytes 663560 | tf_op jit(solution)/shard_map/ppermute | solution.py:27
  134.6 15.0 %collective-permute-start.5 = (f32[8,54,1,128]{3,0,1,2:T(8,128)}, f32[8,54,1,128]{3,0,1,2:T(8,128)}, u32[]{:S(2)}, u32[]{:S(2)}) collective-permute-start(f32[8,54,1,128]{3,0,1,2:T(8,128)} %get-tuple-element.105), channel_id=1, source_target_pairs={{2,0},{4,2},{6,4},{8,6},{10,8},{12,10},{14,12},{0,14},{3,1},{5,3},... | collective-permute-start | bytes 663560 | tf_op jit(solution)/shard_map/ppermute | solution.py:28
  137.0 3.1 %copy-start.14 = (f32[8,1,4,128]{3,0,1,2:T(8,128)S(1)}, f32[8,1,4,128]{3,0,1,2:T(8,128)}, u32[]{:S(2)}) copy-start(f32[8,1,4,128]{3,0,1,2:T(8,128)} %get-tuple-element.103) | copy-start | bytes 49156
  137.0 3.1 %copy-start.15 = (f32[8,1,4,128]{3,0,1,2:T(8,128)S(1)}, f32[8,1,4,128]{3,0,1,2:T(8,128)}, u32[]{:S(2)}) copy-start(f32[8,1,4,128]{3,0,1,2:T(8,128)} %get-tuple-element.104) | copy-start | bytes 49156
  140.8 11.2 %collective-permute-start.9 = (f32[8,2,4,128]{3,0,1,2:T(8,128)}, f32[8,2,4,128]{3,0,1,2:T(8,128)}, u32[]{:S(2)}, u32[]{:S(2)}) collective-permute-start(f32[8,2,4,128]{3,0,1,2:T(8,128)} %pad_maximum_fusion.13), channel_id=1, source_target_pairs={{0,16},{16,0},{1,17},{17,1},{2,18},{18,2},{3,19},{19,3},{4,20},{20... | collective-permute-start | bytes 98312 | tf_op jit(solution)/shard_map/ppermute | solution.py:17
  211.2 4.2 %copy-start.2 = (f32[8,54,4,1]{3,0,1,2:T(8,128)S(1)}, f32[8,54,4,1]{3,0,1,2:T(8,128)}, u32[]{:S(2)}) copy-start(f32[8,54,4,1]{3,0,1,2:T(8,128)} %get-tuple-element.101) | copy-start | bytes 20740
  213.4 15.0 %collective-permute-start.13 = (f32[8,54,4,1]{1,0,3,2:T(8,128)}, f32[8,54,4,1]{1,0,3,2:T(8,128)}, u32[]{:S(2)}, u32[]{:S(2)}) collective-permute-start(f32[8,54,4,1]{1,0,3,2:T(8,128)} %copy.239), channel_id=1, source_target_pairs={{0,1},{2,3},{4,5},{6,7},{8,9},{10,11},{12,13},{14,15},{16,17},{18,... | collective-permute-start | bytes 20744 | tf_op jit(solution)/shard_map/ppermute | solution.py:27
  216.4 13.2 %collective-permute-start.12 = (f32[8,54,4,1]{1,0,3,2:T(8,128)}, f32[8,54,4,1]{1,0,3,2:T(8,128)S(1)}, u32[]{:S(2)}, u32[]{:S(2)}) collective-permute-start(f32[8,54,4,1]{1,0,3,2:T(8,128)} %copy.237), channel_id=1, source_target_pairs={{1,0},{3,2},{5,4},{7,6},{9,8},{11,10},{13,12},{15,14},{17,16},{19,... | collective-permute-start | bytes 20744 | tf_op jit(solution)/shard_map/ppermute | solution.py:28
  217.6 13.4 %collective-permute-start.11 = (f32[8,54,1,128]{3,0,1,2:T(8,128)}, f32[8,54,1,128]{3,0,1,2:T(8,128)S(1)}, u32[]{:S(2)}, u32[]{:S(2)}) collective-permute-start(f32[8,54,1,128]{3,0,1,2:T(8,128)} %get-tuple-element.100), channel_id=1, source_target_pairs={{0,2},{2,4},{4,6},{6,8},{8,10},{10,12},{12,14},{14,0},{1,3},{3,5},... | collective-permute-start | bytes 663560 | tf_op jit(solution)/shard_map/ppermute | solution.py:27
  220.3 13.2 %collective-permute-start.10 = (f32[8,54,1,128]{3,0,1,2:T(8,128)}, f32[8,54,1,128]{3,0,1,2:T(8,128)}, u32[]{:S(2)}, u32[]{:S(2)}) collective-permute-start(f32[8,54,1,128]{3,0,1,2:T(8,128)} %get-tuple-element.99), channel_id=1, source_target_pairs={{2,0},{4,2},{6,4},{8,6},{10,8},{12,10},{14,12},{0,14},{3,1},{5,3},... | collective-permute-start | bytes 663560 | tf_op jit(solution)/shard_map/ppermute | solution.py:28
  226.2 9.8 %collective-permute-start.14 = (f32[8,2,4,128]{3,0,1,2:T(8,128)}, f32[8,2,4,128]{3,0,1,2:T(8,128)}, u32[]{:S(2)}, u32[]{:S(2)}) collective-permute-start(f32[8,2,4,128]{3,0,1,2:T(8,128)} %pad_maximum_fusion.14), channel_id=1, source_target_pairs={{0,16},{16,0},{1,17},{17,1},{2,18},{18,2},{3,19},{19,3},{4,20},{20... | collective-permute-start | bytes 98312 | tf_op jit(solution)/shard_map/ppermute | solution.py:17
  (20 other events, 22.8 us)
